TPU v7x, 512 devices: a 8x2x16 block of a 8x8x16 slice. The times are simulated.
512 devices in a mesh: group: 2 (over y), seq: 32 (over z, core), tensor: 8 (over x).
Axes of the slice: x: 8, y: 2, z: 16, core: 2. Of those that a mesh axis runs over, the one named last changes fastest.
The devices are a block of a 8x8x16 slice.
Arguments:
- query: bfloat16 [128, 7168], P(('group', 'seq'), 'tensor'), parts along dimension 0, may hold values from -5 to 5
- key_cache: bfloat16 [256, 256, 7168], P(('group', 'seq'), None, 'tensor'), parts along dimension 0, may hold values from -5 to 5
- value_cache: bfloat16 [256, 256, 7168], P(('group', 'seq'), None, 'tensor'), parts along dimension 0, may hold values from -6 to 6
- alibi_slopes: float32 [56], P('tensor'), may hold values from 0 to 1, as said below
- block_seq: int32 [256], P(('group', 'seq')), parts along dimension 0, may hold values from 0 to 63, as said below
- block_pos: int32 [256], P(('group', 'seq')), parts along dimension 0, may hold values from 0 to 16, as said below
- lengths: int32 [128], P('group'), parts along dimension 0, may hold values from 1 to 4352, as said below
- out_weight: bfloat16 [7168, 14336], P('tensor', 'seq'), may hold values from -0.5 to 0.5
Outputs:
- mixed: bfloat16 [128, 14336], P(('group', 'tensor'), 'seq'), parts along dimension 0
There are 2 independent parts, one for each index of `group`. A program takes and returns all parts, laid end to end along the dimension named above; an argument that names none is the same for every part. Nothing has to cross between parts.
Inputs may be any that keep to these rules, and one draw needn't show every extreme that they name: `block_seq`: every sequence owns at least one block and at most 17; the blocks of sequence s have block_pos 0 to n_s - 1, each once. block_pos of a block is below the number of blocks its sequence owns. `lengths`: A sequence that owns n blocks has a length above 256 * (n - 1) and at most 256 * n. `alibi_slopes`: positive slopes.
All inputs are finite; a program needn't handle non-finite values.
Results may differ from a plain program's by a relative error of at most 0.0054.
Values may be sent and summed in bfloat16 or wider, within the bound.
A program may use at most 64 MiB of HBM per device.

v0:
```python
import math

import jax
import jax.numpy as jnp
from jax import lax
from jax.sharding import PartitionSpec as P


def joined_along(parts, dim):
    parts = jnp.moveaxis(parts, 0, dim)
    dims = parts.shape
    return parts.reshape(*dims[:dim], dims[dim] * dims[dim + 1], *dims[dim + 2 :])


def sent_to_all(x, axis):
    copies = jnp.broadcast_to(x, (lax.axis_size(axis), *x.shape))
    return lax.all_to_all(copies, axis, split_axis=0, concat_axis=0, tiled=True)


def gathered_copies(x, axis, dim):
    return joined_along(sent_to_all(x, axis), dim)


def side_by_side(arrays, axis, split_dim, concat_dim, along):
    columns = [a.reshape(*a.shape[:along], -1) for a in arrays]
    both = jnp.concatenate(columns, axis=along)
    result, at, outs = (
        lax.all_to_all(both, axis, split_axis=split_dim, concat_axis=concat_dim, tiled=True),
        0,
        [],
    )
    for a, column in zip(arrays, columns):
        slab = result[..., at : at + column.shape[along]]
        outs.append(slab.reshape(*slab.shape[:along], *a.shape[along:]))
        at += column.shape[along]
    return tuple(outs)


def in_blocks(x, dim, length):
    before, after = (x.shape[:dim], x.shape[dim + 1 :])
    return jnp.moveaxis(x.reshape(*before, length, -1, *after), dim, 0)


def summed_on_arrival(x, axis, dim):
    length = lax.axis_size(axis)
    parts = lax.all_to_all(in_blocks(x, dim, length), axis, 0, 0, tiled=True)
    return jnp.sum(parts, axis=0)


def local(query, key_cache, value_cache, alibi_slopes, block_seq, block_pos, lengths, out_weight):
    heads = alibi_slopes.shape[0]
    features = query.shape[1]
    head_size = features // heads
    blocks_here = key_cache.shape[0]
    block_len = key_cache.shape[1]
    seq_count = lengths.shape[0]
    scale = 1.0 / math.sqrt(head_size)
    whole_query = gathered_copies(query, "seq", 0)
    query_rows = jnp.take(whole_query, block_seq, axis=0).reshape(blocks_here, heads, head_size)
    keys = key_cache.reshape(blocks_here, block_len, heads, head_size)
    values = value_cache.reshape(blocks_here, block_len, heads, head_size)
    scores = (
        jnp.einsum("bthd,bhd->bht", keys, query_rows, preferred_element_type=jnp.float32) * scale
    )
    owner_length = lengths[block_seq]
    placed = block_pos[:, None] * block_len + jnp.arange(block_len, dtype=jnp.int32)[None, :]
    live = (placed < owner_length[:, None])[:, None, :]
    distance = (owner_length[:, None] - 1 - placed).astype(jnp.float32)
    scores = scores - alibi_slopes[None, :, None] * distance[:, None, :]
    scores = jnp.where(live, scores, -1e30)
    block_top = jnp.max(scores, axis=2)
    weights = jnp.where(live, jnp.exp(scores - block_top[:, :, None]), 0.0)
    block_total = jnp.sum(weights, axis=2)
    block_acc = jnp.einsum(
        "bht,bthd->bhd", weights.astype(jnp.bfloat16), values, preferred_element_type=jnp.float32
    )
    seq_ids = jnp.arange(seq_count, dtype=jnp.int32)
    owned = (block_seq[None, :] == seq_ids[:, None])[:, :, None]
    local_top = jnp.max(jnp.where(owned, block_top[None], -1e30), axis=1)
    factor = jnp.where(owned, jnp.exp(block_top[None] - local_top[:, None, :]), 0.0)
    local_total = jnp.sum(factor * block_total[None], axis=1)
    local_acc = jnp.einsum("sbh,bhd->shd", factor, block_acc, precision=lax.Precision.HIGHEST)
    tops, totals, accs = side_by_side(
        (local_top[None], local_total[None], local_acc[None]), "seq", 1, 0, 3
    )
    best = jnp.max(tops, axis=0)
    scaling = jnp.exp(tops - best[None])
    home_total = jnp.sum(totals * scaling, axis=0)
    home_acc = jnp.sum(accs * scaling[..., None], axis=0)
    mine = (
        (home_acc / home_total[:, :, None])
        .astype(jnp.bfloat16)
        .reshape(home_acc.shape[0], features)
    )
    attention = gathered_copies(mine, "seq", 0)
    mixed = summed_on_arrival(
        jnp.dot(attention, out_weight, preferred_element_type=jnp.float32), "tensor", 0
    )
    return mixed.astype(jnp.bfloat16)


def solution(mesh):
    placed = (
        P(("group", "seq"), "tensor"),
        P(("group", "seq"), None, "tensor"),
        P(("group", "seq"), None, "tensor"),
        P("tensor"),
        P(("group", "seq")),
        P(("group", "seq")),
        P("group"),
        P("tensor", "seq"),
    )
    return jax.shard_map(
        local, mesh=mesh, in_specs=placed, out_specs=P(("group", "tensor"), "seq"), check_vma=False
    )
```

profile of v0, /device:TPU:65, one launch (start us, length us, event | category | flops | bytes accessed | tf_op | source)
XLA Modules:
  0.0 140.8 jit_solution(4068384018980198913)
XLA Ops:
  0.0 1.5 %broadcast_in_dim.92 = bf16[32,2,896]{2,1,0:T(2,128)(2,1)} broadcast(bf16[2,896]{1,0:T(2,128)(2,1)} %param.8), dimensions={1,2} | broadcast | bytes 118272 | tf_op jit(solution)/shard_map/broadcast_in_dim | solution.py:16
  1.5 45.2 %all-to-all-start = ((bf16[32,2,896]{2,1,0:T(2,128)(2,1)}), bf16[32,2,896]{2,1,0:T(2,128)(2,1)S(1)}, u32[]{:S(2)}, u32[]{:S(2)}) async-start(bf16[32,2,896]{2,1,0:T(2,128)(2,1)} %broadcast_in_dim.92), calls=%async_computation | async-start | bytes 229376 | tf_op jit(solution)/shard_map/all_to_all | solution.py:17
  46.6 0.7 compare_select_fusion
  47.3 0.7 compare_and_fusion
  48.0 1.3 gather_fusion
  49.3 0.7 broadcast_add_fusion
  50.0 3.5 %copy.68 = bf16[4,256,896]{1,2,0:T(8,128)(2,1)} copy(bf16[4,256,896]{2,1,0:T(8,128)(2,1)} %param.9) | data formatting | bytes 3670016 | tf_op args[1]
  53.6 2.8 %copy.69 = bf16[4,256,896]{1,2,0:T(8,128)(2,1)S(1)} copy(bf16[4,256,896]{2,1,0:T(8,128)(2,1)} %param.10) | data formatting | bytes 3670016 | tf_op args[2]
  56.5 5.5 %all-to-all-done = bf16[32,2,896]{2,1,0:T(2,128)(2,1)S(1)} async-done(((bf16[32,2,896]{2,1,0:T(2,128)(2,1)}), bf16[32,2,896]{2,1,0:T(2,128)(2,1)S(1)}, u32[]{:S(2)}, u32[]{:S(2)}) %all-to-all-start) | async-done | bytes 114720 | tf_op jit(solution)/shard_map/all_to_all | solution.py:17
  62.0 0.6 gather_fusion.1
  62.7 1.8 %fusion.12 = f32[4,7,1,256]{3,2,1,0:T(1,128)S(1)} fusion(bf16[4,256,7,128]{1,3,2,0:T(8,128)(2,1)} %bitcast.44, bf16[4,7,128,1]{2,1,0,3:T(8,128)(2,1)S(1)} %select_bitcast_fusion), kind=kOutput, calls=%fused_computation.19 | convolution fusion | flops 1835008 | bytes 1870848 | tf_op jit(solution)/shard_map/bthd,bhd->bht/dot_general | solution.py:63
  64.7 0.2 fusion.8
  65.2 0.6 fusion.5
  65.8 0.7 convolution_bitcast_fusion
  66.6 0.3 pad_maximum_fusion
  66.9 0.5 copy.72
  67.4 37.5 %all_to_all.27 = f32[1,64,7,130]{3,0,2,1:T(1,128)S(1)} all-to-all(f32[1,64,7,130]{3,0,2,1:T(1,128)S(1)} %copy.72), channel_id=1, replica_groups=mesh['group'=2,'seq'=32,'tensor'=8] {'seq'}, dimensions={1} | all-to-all | bytes 465920 | tf_op jit(solution)/shard_map/all_to_all | solution.py:28
  105.3 0.2 copy.76
  105.4 0.2 copy.85
  106.1 0.3 fusion.2
  106.6 18.7 %all_to_all.28 = bf16[32,2,896]{2,1,0:T(2,128)(2,1)S(1)} all-to-all(bf16[32,2,896]{2,1,0:T(2,128)(2,1)S(1)} %broadcast_in_dim.100), channel_id=1, replica_groups=mesh['group'=2,'seq'=32,'tensor'=8] {'seq'}, dimensions={0} | all-to-all | bytes 229376 | tf_op jit(solution)/shard_map/all_to_all | solution.py:17
  125.3 0.4 fusion
  125.7 14.5 %all_to_all.29 = f32[8,8,448]{2,1,0:T(8,128)S(1)} all-to-all(f32[8,8,448]{2,1,0:T(8,128)S(1)} %fusion), channel_id=1, replica_groups=mesh['group'=2,'seq'=32,'tensor'=8] {'tensor'}, dimensions={0} | all-to-all | bytes 229376 | tf_op jit(solution)/shard_map/all_to_all | solution.py:46
  140.2 0.6 reduce_sum.49
  (28 shorter events, 2.0 us)
Async XLA Ops:
  0.0 125.3 %copy-start = (bf16[896,448]{0,1:T(8,128)(2,1)S(1)}, bf16[896,448]{0,1:T(8,128)(2,1)}, u32[]{:S(2)}) copy-start(bf16[896,448]{0,1:T(8,128)(2,1)} %param.15) | copy-start | bytes 2408452
  1.5 60.5 %all-to-all-start = ((bf16[32,2,896]{2,1,0:T(2,128)(2,1)}), bf16[32,2,896]{2,1,0:T(2,128)(2,1)S(1)}, u32[]{:S(2)}, u32[]{:S(2)}) async-start(bf16[32,2,896]{2,1,0:T(2,128)(2,1)} %broadcast_in_dim.92), calls=%async_computation | async-start | bytes 229376 | tf_op jit(solution)/shard_map/all_to_all | solution.py:17
  53.5 2.8 %copy-start.2 = (s32[4]{0:T(128)S(1)}, s32[4]{0:T(128)}, u32[]{:S(2)}) copy-start(s32[4]{0:T(128)} %param.12) | copy-start | bytes 52
  56.3 8.2 %copy-start.1 = (f32[7]{0:T(128)S(1)}, f32[7]{0:T(128)}, u32[]{:S(2)}) copy-start(f32[7]{0:T(128)} %param.11) | copy-start | bytes 88
where the time goes:
time: 143 us; the launch traced here: 141 us
  blocking collectives  70.7 us (49%)
  starting transfers between devices  45.2 us (32%)
  local copies, waits for them, and re-layouts  11.3 us (8%)
  waiting for transfers between devices  5.48 us (4%)
  other arithmetic  4.52 us (3%)
  matrix products  3.46 us (2%)
    all_to_all x1, starting transfers between devices, sent_to_all(): return lax.all_to_all(copies, axis, split_axis=0, concat_axis=0, tiled=True)  45.2 us
    all_to_all x1, blocking collectives, side_by_side(): lax.all_to_all(both, axis, split_axis=split_dim, concat_axis=concat_dim,...  37.5 us
    all_to_all x1, blocking collectives, sent_to_all(): return lax.all_to_all(copies, axis, split_axis=0, concat_axis=0, tiled=True)  18.7 us
    all_to_all x1, blocking collectives, summed_on_arrival(): parts = lax.all_to_all(in_blocks(x, dim, length), axis, 0, 0, tiled=True)  14.5 us
    unnamed x11, local copies, waits for them, and re-layouts  6.65 us
    all_to_all x1, waiting for transfers between devices, sent_to_all(): return lax.all_to_all(copies, axis, split_axis=0, concat_axis=0, tiled=True)  5.48 us
  transfers between devices with their start and end apart: 1, of which 1 were waited for; matrix products, arithmetic and copies ran while one was open for 7% of the time, Pallas kernels for 0%

commit v1 on v0

v1 whole, which is shorter than its diff:
```python
import functools
import math

import jax
import jax.numpy as jnp
from jax import lax
from jax.experimental import pallas as pl
from jax.experimental.pallas import tpu as pltpu
from jax.sharding import PartitionSpec as P

MESH = pl.DeviceIdType.MESH
F32 = jnp.float32
BF16 = jnp.bfloat16
CORES = 2
GONE = -1e30


def remote(src, dst, send, recv, where):
    return pltpu.make_async_remote_copy(
        src_ref=src, dst_ref=dst, send_sem=send, recv_sem=recv, device_id=where, device_id_type=MESH
    )


def spread(slots, chips, z, c, send, recv, relay):
    def copy(k):
        there = lax.rem(z + k, chips) * CORES + c
        return remote(slots.at[c, z], slots.at[c, z], send.at[k], recv.at[k], {"seq": there})

    def start(i, _):
        far = chips // 2
        step = (i + 1) // 2
        k = jnp.where(lax.rem(i, 2) == 0, far - step, far + step)
        copy(k).start()
        return 0

    lax.fori_loop(0, chips - 1, start, 0)

    def arrive(k, _):
        copy(k).wait_recv()
        return 0

    lax.fori_loop(1, chips, arrive, 0)
    half = remote(slots.at[c], slots.at[c], relay.at[0], relay.at[1], {"seq": z * CORES + (1 - c)})
    half.start()
    half.wait_recv()

    def drain():
        def sent(k, _):
            copy(k).wait_send()
            return 0

        lax.fori_loop(1, chips, sent, 0)
        half.wait_send()

    return drain


def kernel(
    chips, owners, heads,
    q_hbm, k_hbm, v_hbm, slopes, block_seq, block_pos, lengths, w_hbm, out,
    kbuf, vbuf, wbuf, qall, gall, part, landed,
    load, q_send, q_recv, q_relay, g_send, g_recv, g_relay, p_send, p_recv,
):
    seq = lax.axis_index("seq")
    mine = lax.axis_index("tensor")
    z, c = seq // CORES, lax.rem(seq, CORES)
    blocks, block_len, features = k_hbm.shape
    rows = q_hbm.shape[0]
    head_dim = features // heads
    seqs = lengths.shape[0]
    scale = 1.0 / math.sqrt(head_dim)

    barrier = pltpu.get_barrier_semaphore()

    def greet_chip(k, _):
        there = lax.rem(z + k, chips) * CORES + c
        pl.semaphore_signal(barrier, inc=1, device_id={"seq": there}, device_id_type=MESH)
        return 0

    def greet_owner(k, _):
        there = lax.rem(mine + k, owners)
        pl.semaphore_signal(barrier, inc=1, device_id={"tensor": there}, device_id_type=MESH)
        return 0

    lax.fori_loop(1, chips, greet_chip, 0)
    pl.semaphore_signal(
        barrier, inc=1, device_id={"seq": z * CORES + (1 - c)}, device_id_type=MESH
    )
    lax.fori_loop(1, owners, greet_owner, 0)

    q_load = pltpu.make_async_copy(q_hbm, qall.at[c, z], load.at[0])
    k_load = pltpu.make_async_copy(k_hbm, kbuf, load.at[1])
    v_load = pltpu.make_async_copy(v_hbm, vbuf, load.at[2])
    w_load = pltpu.make_async_copy(w_hbm, wbuf, load.at[3])
    q_load.start()
    k_load.start()
    v_load.start()
    w_load.start()
    q_load.wait()
    pl.semaphore_wait(barrier, chips - 1 + 1 + owners - 1)

    q_drain = spread(qall, chips, z, c, q_send, q_recv, q_relay)

    sub = lax.broadcasted_iota(jnp.int32, (8, features), 0)
    lane = lax.broadcasted_iota(jnp.int32, (8, features), 1)
    own_head = lane // head_dim == sub
    t_at = lax.broadcasted_iota(jnp.int32, (8, block_len), 1)
    h_at = lax.broadcasted_iota(jnp.int32, (8, block_len), 0)
    slope = jnp.zeros((8, block_len), F32)
    for h in range(heads):
        slope = jnp.where(h_at == h, slopes[h], slope)
    a_sub = lax.broadcasted_iota(jnp.int32, (8, head_dim), 0)
    a_lane = lax.broadcasted_iota(jnp.int32, (8, head_dim), 1)

    k_load.wait()
    v_load.wait()
    wholes = []
    for b in range(blocks):
        s = block_seq[b]
        length = lengths[s]
        owner = s // rows
        r = lax.rem(s, rows)
        pair = qall[lax.rem(owner, CORES), owner // CORES].astype(F32)
        row = pair[0:1]
        for i in range(1, rows):
            row = jnp.where(r == i, pair[i : i + 1], row)
        wide = jnp.where(own_head, jnp.broadcast_to(row, (8, features)), 0.0).astype(BF16)
        scores = lax.dot_general(
            wide, kbuf[b], (((1,), (1,)), ((), ())), preferred_element_type=F32
        )
        placed = block_pos[b] * block_len + t_at
        live = placed < length
        distance = (length - 1 - placed).astype(F32)
        scores = jnp.where(live, scores * scale - slope * distance, GONE)
        top = jnp.max(scores, axis=1, keepdims=True)
        weights = jnp.where(live, jnp.exp(scores - top), 0.0)
        total = jnp.sum(weights, axis=1, keepdims=True)
        acc = jnp.dot(weights.astype(BF16), vbuf[b], preferred_element_type=F32)
        o = jnp.sum(jnp.where(own_head, acc / total, 0.0), axis=0, keepdims=True)
        lse = top + jnp.log(total)
        high = lse.astype(BF16).astype(F32)
        mid = (lse - high).astype(BF16).astype(F32)
        low = lse - high - mid
        tail = jnp.where(a_lane == a_sub, high, 0.0)
        tail = jnp.where(a_lane == a_sub + 8, mid, tail)
        tail = jnp.where(a_lane == a_sub + 16, low, tail)
        tail = jnp.where((a_lane == 24) & (a_sub == 0), s.astype(F32), tail)
        tail = jnp.sum(jnp.where(a_sub < heads, tail, 0.0), axis=0, keepdims=True)
        wholes.append(jnp.concatenate([o, tail], axis=1))

    wide = 2 * head_dim
    groups = (heads + 1) // 2
    m_sub = lax.broadcasted_iota(jnp.int32, (8, wide), 0)
    halves = []
    for first in range(0, groups * blocks, 8):
        half = jnp.zeros((8, wide), F32)
        for i in range(8):
            j, b = divmod(first + i, blocks)
            piece = wholes[b][:, j * wide : (j + 1) * wide]
            half = jnp.where(m_sub == i, jnp.broadcast_to(piece, (8, wide)), half)
        halves.append(half)
    gall[c, z] = jnp.concatenate(halves, axis=0).astype(BF16)

    g_drain = spread(gall, chips, z, c, g_send, g_recv, g_relay)

    high_rows = groups * blocks
    count = CORES * chips * high_rows
    both = gall[...].reshape(count, wide)
    p_sub = lax.broadcasted_iota(jnp.int32, (16, head_dim), 0)
    p_lane = lax.broadcasted_iota(jnp.int32, (16, head_dim), 1)
    pick = (p_sub < 8) & (p_lane < 24) & (lax.rem(p_lane, 8) == p_sub)
    pick = pick | ((p_sub == 8) & (p_lane == 24))
    pick = jnp.where(pick, 1.0, 0.0).astype(BF16)
    tails = lax.dot_general(
        pick, both[:, head_dim:], (((1,), (1,)), ((), ())), preferred_element_type=F32
    )
    column = lax.broadcasted_iota(jnp.int32, (seqs, count), 1)
    group_of = lax.rem(column // blocks, groups)
    seq_at = lax.broadcasted_iota(jnp.int32, (seqs, count), 0).astype(F32)
    shares = []
    for j in range(groups):
        back = (groups - 1 - j) * blocks
        moved = tails if back == 0 else pltpu.roll(tails, count - back, 1)
        mask = (group_of == j) & (jnp.broadcast_to(moved[8:9], (seqs, count)) == seq_at)
        for h in range(2 * j, min(2 * j + 2, heads)):
            level = jnp.where(mask, jnp.broadcast_to(moved[h : h + 1], (seqs, count)), GONE)
            best = jnp.max(level, axis=1, keepdims=True)
            share = jnp.exp(level - best)
            share = share / jnp.sum(share, axis=1, keepdims=True)
            shares.append(share.astype(BF16))
    mixed = jnp.dot(jnp.concatenate(shares, axis=0), both, preferred_element_type=F32)
    attention = jnp.concatenate(
        [
            mixed[h * seqs : (h + 1) * seqs, (h % 2) * head_dim : (h % 2 + 1) * head_dim].astype(BF16)
            for h in range(heads)
        ],
        axis=1,
    )
    w_load.wait()
    product = jnp.dot(attention, wbuf[...], preferred_element_type=F32)
    share_rows = seqs // owners
    for x in range(owners):
        part[x] = product[x * share_rows : (x + 1) * share_rows].astype(BF16)

    def give(k):
        there = lax.rem(mine + k, owners)
        return remote(part.at[there], landed.at[k], p_send.at[k], p_recv.at[k], {"tensor": there})

    def give_start(i, _):
        far = owners // 2
        step = (i + 1) // 2
        give(jnp.where(lax.rem(i, 2) == 0, far - step, far + step)).start()
        return 0

    lax.fori_loop(0, owners - 1, give_start, 0)
    result = part[mine].astype(F32)

    def give_arrive(k, _):
        give(k).wait_recv()
        return 0

    lax.fori_loop(1, owners, give_arrive, 0)
    for k in range(1, owners):
        result = result + landed[k].astype(F32)
    out[...] = result.astype(BF16)

    q_drain()
    g_drain()

    def give_sent(k, _):
        give(k).wait_send()
        return 0

    lax.fori_loop(1, owners, give_sent, 0)


def solution(mesh):
    chips = mesh.shape["seq"] // CORES
    owners = mesh.shape["tensor"]

    def local(query, key_cache, value_cache, alibi_slopes, block_seq, block_pos, lengths, out_weight):
        heads = alibi_slopes.shape[0]
        rows, features = query.shape
        blocks, block_len, _ = key_cache.shape
        seqs = lengths.shape[0]
        columns = out_weight.shape[1]
        head_dim = features // heads
        message = ((heads + 1) // 2 * blocks, 2 * head_dim)
        smem = pl.BlockSpec(memory_space=pltpu.SMEM)
        hbm = pl.BlockSpec(memory_space=pl.ANY)
        dma = pltpu.SemaphoreType.DMA
        return pl.pallas_call(
            functools.partial(kernel, chips, owners, heads),
            out_shape=jax.ShapeDtypeStruct((seqs // owners, columns), BF16),
            in_specs=[hbm, hbm, hbm, smem, smem, smem, smem, hbm],
            out_specs=pl.BlockSpec(memory_space=pltpu.VMEM),
            scratch_shapes=[
                pltpu.VMEM(key_cache.shape, BF16),
                pltpu.VMEM(value_cache.shape, BF16),
                pltpu.VMEM(out_weight.shape, BF16),
                pltpu.VMEM((CORES, chips, rows, features), BF16),
                pltpu.VMEM((CORES, chips, *message), BF16),
                pltpu.VMEM((owners, seqs // owners, columns), BF16),
                pltpu.VMEM((owners, seqs // owners, columns), BF16),
                dma((4,)),
                dma((chips,)),
                dma((chips,)),
                dma((2,)),
                dma((chips,)),
                dma((chips,)),
                dma((2,)),
                dma((owners,)),
                dma((owners,)),
            ],
            compiler_params=pltpu.CompilerParams(
                collective_id=0, has_side_effects=True, vmem_limit_bytes=32 * 1024 * 1024
            ),
        )(query, key_cache, value_cache, alibi_slopes, block_seq, block_pos, lengths, out_weight)

    placed = (
        P(("group", "seq"), "tensor"),
        P(("group", "seq"), None, "tensor"),
        P(("group", "seq"), None, "tensor"),
        P("tensor"),
        P(("group", "seq")),
        P(("group", "seq")),
        P("group"),
        P("tensor", "seq"),
    )
    return jax.shard_map(
        local, mesh=mesh, in_specs=placed, out_specs=P(("group", "tensor"), "seq"), check_vma=False
    )
```

time: 143 us -> 85.4 us (0.60); the launches traced: 141 us -> 84.6 us
  Pallas kernels: 0 us -> 76.2 us
  blocking collectives: 70.7 us -> 0 us
  starting transfers between devices: 45.2 us -> 0 us
  waiting for transfers between devices: 5.48 us -> 0 us
  other arithmetic: 4.52 us -> 0 us
  matrix products: 3.46 us -> 0 us
  local copies, waits for them, and re-layouts: 11.3 us -> 8.35 us
    pallas_call x0 -> x1, Pallas kernels: none -> 76.2 us  [local(): pl.pallas_call(functools.partial(kernel, chips, owners, heads), out_shape...]
    all_to_all x3 -> x0, blocking collectives: 70.7 us -> none  [the longest x1 37.5 us: side_by_side(): lax.all_to_all(both, axis, split_axis=split_dim, concat_axis=concat_dim,...]
    all_to_all x1 -> x0, starting transfers between devices: 45.2 us -> none  [sent_to_all(): return lax.all_to_all(copies, axis, split_axis=0, concat_axis=0, tiled=True)]
    all_to_all x1 -> x0, waiting for transfers between devices: 5.48 us -> none  [sent_to_all(): return lax.all_to_all(copies, axis, split_axis=0, concat_axis=0, tiled=True)]
    dot_general x4 -> x0, matrix products: 3.46 us -> none  [the longest x1 1.84 us: local(): jnp.einsum('bthd,bhd->bht', keys, query_rows, preferred_element_type=jnp....]
    gather x3 -> x0, local copies, waits for them, and re-layouts: 1.89 us -> none  [the longest x1 1.3 us: local(): owner_length = lengths[block_seq]]
    unnamed x11 -> x16, local copies, waits for them, and re-layouts: 6.65 us -> 8.35 us
    broadcast_in_dim x2 -> x0, local copies, waits for them, and re-layouts: 1.52 us -> none  [sent_to_all(): copies = jnp.broadcast_to(x, (lax.axis_size(axis), *x.shape))]
  transfers between devices with their start and end apart: 1 -> 0, of which waited for: 1 -> 0; matrix products, arithmetic and copies ran while one was open for 7% -> 0% of each run, Pallas kernels for 0% -> 0%
where the time goes in v1:
time: 85.4 us; the launch traced here: 84.6 us
  Pallas kernels  76.2 us (89%)
  local copies, waits for them, and re-layouts  8.35 us (10%)
    pallas_call x1, Pallas kernels, local(): pl.pallas_call(functools.partial(kernel, chips, owners, heads), out_shape...  76.2 us
    unnamed x16, local copies, waits for them, and re-layouts  8.35 us

profile of v1, /device:TPU:65, one launch (start us, length us, event | category | flops | bytes accessed | tf_op | source)
XLA Modules:
  0.0 84.6 jit_solution(4633395869269900799)
XLA Ops:
  0.0 1.5 %copy.9.w_hbm = bf16[896,448]{1,0:T(8,128)(2,1)S(1)} copy(bf16[896,448]{0,1:T(8,128)(2,1)} %param.15) | data formatting | bytes 1605632 | tf_op args[7]
  1.5 0.0 copy-start
  1.5 1.5 %copy-done = bf16[4,256,896]{2,1,0:T(8,128)(2,1)S(1)} copy-done((bf16[4,256,896]{2,1,0:T(8,128)(2,1)S(1)}, bf16[4,256,896]{2,1,0:T(8,128)(2,1)}, u32[]{:S(2)}) %copy-start) | copy-done | bytes 1835032
  3.0 0.0 copy-start.1
  3.0 1.5 %copy-done.1 = bf16[4,256,896]{2,1,0:T(8,128)(2,1)S(1)} copy-done((bf16[4,256,896]{2,1,0:T(8,128)(2,1)S(1)}, bf16[4,256,896]{2,1,0:T(8,128)(2,1)}, u32[]{:S(2)}) %copy-start.1) | copy-done | bytes 1835032
  4.5 0.0 copy-start.2
  4.5 0.7 copy-done.2
  5.2 0.0 copy-start.3
  5.2 0.7 copy-done.3
  5.8 0.0 copy-start.4
  5.8 0.7 copy-done.4
  6.5 0.0 copy-start.5
  6.5 0.7 copy-done.5
  7.1 0.0 copy-start.6
  7.1 0.7 copy-done.6
  7.8 76.2 %shard_map.82 = bf16[8,448]{1,0:T(8,128)(2,1)S(1)} custom-call(bf16[2,896]{1,0:T(2,128)(2,1)S(1)} %copy-done.2, bf16[4,256,896]{2,1,0:T(8,128)(2,1)S(1)} %copy-done, bf16[4,256,896]{2,1,0:T(8,128)(2,1)S(1)} %copy-done.1, f32[7]{0:T(128)S(1)} %copy-done.3, s32[4]{0:T(128)S(1)} %copy-done.4, s32[4]{0:T(128)S(1)} %copy-done.5, s32[64]{0:T(128)S(1)} %copy-done.6, ...), custom_call_target="tpu_custom_call" | custom-call | tf_op jit(solution)/shard_map/pallas_call | solution.py:252
  84.0 0.6 copy.11
Async XLA Ops:
  1.5 1.5 %copy-start = (bf16[4,256,896]{2,1,0:T(8,128)(2,1)S(1)}, bf16[4,256,896]{2,1,0:T(8,128)(2,1)}, u32[]{:S(2)}) copy-start(bf16[4,256,896]{2,1,0:T(8,128)(2,1)} %k_hbm.1) | copy-start | bytes 5505028
  3.0 1.5 %copy-start.1 = (bf16[4,256,896]{2,1,0:T(8,128)(2,1)S(1)}, bf16[4,256,896]{2,1,0:T(8,128)(2,1)}, u32[]{:S(2)}) copy-start(bf16[4,256,896]{2,1,0:T(8,128)(2,1)} %v_hbm.1) | copy-start | bytes 5505028
  4.5 0.7 copy-start.2
  5.2 0.7 copy-start.3
  5.8 0.7 copy-start.4
  6.5 0.7 copy-start.5
  7.1 0.7 copy-start.6

commit v2 on v1

--- a/solution.py
+++ b/solution.py
@@ -57,8 +57,8 @@
 
 def kernel(
     chips, owners, heads,
-    q_hbm, k_hbm, v_hbm, slopes, block_seq, block_pos, lengths, w_hbm, out,
-    kbuf, vbuf, wbuf, qall, gall, part, landed,
+    q_hbm, k_hbm, v_hbm, slopes_hbm, block_seq_hbm, block_pos_hbm, lengths_hbm, w_hbm, out,
+    slopes, block_seq, block_pos, lengths, kbuf, vbuf, wbuf, qall, gall, part, landed,
     load, q_send, q_recv, q_relay, g_send, g_recv, g_relay, p_send, p_recv,
 ):
     seq = lax.axis_index("seq")
@@ -67,7 +67,7 @@
     blocks, block_len, features = k_hbm.shape
     rows = q_hbm.shape[0]
     head_dim = features // heads
-    seqs = lengths.shape[0]
+    seqs = lengths_hbm.shape[0]
     scale = 1.0 / math.sqrt(head_dim)
 
     barrier = pltpu.get_barrier_semaphore()
@@ -92,7 +92,20 @@
     k_load = pltpu.make_async_copy(k_hbm, kbuf, load.at[1])
     v_load = pltpu.make_async_copy(v_hbm, vbuf, load.at[2])
     w_load = pltpu.make_async_copy(w_hbm, wbuf, load.at[3])
+    small = [
+        pltpu.make_async_copy(src, dst, load.at[4 + i])
+        for i, (src, dst) in enumerate(
+            (
+                (slopes_hbm, slopes),
+                (block_seq_hbm, block_seq),
+                (block_pos_hbm, block_pos),
+                (lengths_hbm, lengths),
+            )
+        )
+    ]
     q_load.start()
+    for copy in small:
+        copy.start()
     k_load.start()
     v_load.start()
     w_load.start()
@@ -106,14 +119,16 @@
     own_head = lane // head_dim == sub
     t_at = lax.broadcasted_iota(jnp.int32, (8, block_len), 1)
     h_at = lax.broadcasted_iota(jnp.int32, (8, block_len), 0)
+    a_sub = lax.broadcasted_iota(jnp.int32, (8, head_dim), 0)
+    a_lane = lax.broadcasted_iota(jnp.int32, (8, head_dim), 1)
+
+    k_load.wait()
+    v_load.wait()
+    for copy in small:
+        copy.wait()
     slope = jnp.zeros((8, block_len), F32)
     for h in range(heads):
         slope = jnp.where(h_at == h, slopes[h], slope)
-    a_sub = lax.broadcasted_iota(jnp.int32, (8, head_dim), 0)
-    a_lane = lax.broadcasted_iota(jnp.int32, (8, head_dim), 1)
-
-    k_load.wait()
-    v_load.wait()
     wholes = []
     for b in range(blocks):
         s = block_seq[b]
@@ -197,7 +212,9 @@
         axis=1,
     )
     w_load.wait()
-    product = jnp.dot(attention, wbuf[...], preferred_element_type=F32)
+    product = lax.dot_general(
+        attention, wbuf[...], (((1,), (1,)), ((), ())), preferred_element_type=F32
+    )
     share_rows = seqs // owners
     for x in range(owners):
         part[x] = product[x * share_rows : (x + 1) * share_rows].astype(BF16)
@@ -246,23 +263,26 @@
         columns = out_weight.shape[1]
         head_dim = features // heads
         message = ((heads + 1) // 2 * blocks, 2 * head_dim)
-        smem = pl.BlockSpec(memory_space=pltpu.SMEM)
-        hbm = pl.BlockSpec(memory_space=pl.ANY)
+        hbm = pl.BlockSpec(memory_space=pltpu.HBM)
         dma = pltpu.SemaphoreType.DMA
         return pl.pallas_call(
             functools.partial(kernel, chips, owners, heads),
             out_shape=jax.ShapeDtypeStruct((seqs // owners, columns), BF16),
-            in_specs=[hbm, hbm, hbm, smem, smem, smem, smem, hbm],
+            in_specs=[hbm] * 8,
             out_specs=pl.BlockSpec(memory_space=pltpu.VMEM),
             scratch_shapes=[
+                pltpu.SMEM(alibi_slopes.shape, F32),
+                pltpu.SMEM(block_seq.shape, jnp.int32),
+                pltpu.SMEM(block_pos.shape, jnp.int32),
+                pltpu.SMEM(lengths.shape, jnp.int32),
                 pltpu.VMEM(key_cache.shape, BF16),
                 pltpu.VMEM(value_cache.shape, BF16),
-                pltpu.VMEM(out_weight.shape, BF16),
+                pltpu.VMEM(out_weight.shape[::-1], BF16),
                 pltpu.VMEM((CORES, chips, rows, features), BF16),
                 pltpu.VMEM((CORES, chips, *message), BF16),
                 pltpu.VMEM((owners, seqs // owners, columns), BF16),
                 pltpu.VMEM((owners, seqs // owners, columns), BF16),
-                dma((4,)),
+                dma((8,)),
                 dma((chips,)),
                 dma((chips,)),
                 dma((2,)),
@@ -273,9 +293,9 @@
                 dma((owners,)),
             ],
             compiler_params=pltpu.CompilerParams(
-                collective_id=0, has_side_effects=True, vmem_limit_bytes=32 * 1024 * 1024
+                collective_id=0, has_side_effects=True
             ),
-        )(query, key_cache, value_cache, alibi_slopes, block_seq, block_pos, lengths, out_weight)
+        )(query, key_cache, value_cache, alibi_slopes, block_seq, block_pos, lengths, out_weight.T)
 
     placed = (
         P(("group", "seq"), "tensor"),

time: 85.4 us -> 78.3 us (0.917)
  local copies, waits for them, and re-layouts: 8.35 us -> 1.3 us
    unnamed x16 -> x1, local copies, waits for them, and re-layouts: 8.35 us -> 1.3 us
where the time goes in v2:
time: 78.3 us; the launch traced here: 77.6 us
  Pallas kernels  76.3 us (97%)
  local copies, waits for them, and re-layouts  1.3 us (2%)
    pallas_call x1, Pallas kernels, local(): pl.pallas_call(functools.partial(kernel, chips, owners, heads), out_shape...  76.3 us

profile of v2, /device:TPU:65, one launch (start us, length us, event | category | flops | bytes accessed | tf_op | source)
XLA Modules:
  0.0 77.6 jit_solution(6116132817749364975)
XLA Ops:
  0.0 76.3 %shard_map.82 = bf16[8,448]{1,0:T(8,128)(2,1)} custom-call(bf16[2,896]{1,0:T(2,128)(2,1)} %q_hbm.1, bf16[4,256,896]{2,1,0:T(8,128)(2,1)} %k_hbm.1, bf16[4,256,896]{2,1,0:T(8,128)(2,1)} %v_hbm.1, f32[7]{0:T(128)} %slopes_hbm.1, s32[4]{0:T(128)} %block_seq_hbm.1, s32[4]{0:T(128)} %block_pos_hbm.1, s32[64]{0:T(128)} %lengths_hbm.1, bf16[448,896]{1,0:T(8,128)(2,1)} %bitcast.1), custom_call_target="tpu_custom_call" | custom-call | tf_op jit(solution)/shard_map/pallas_call | solution.py:268
  76.3 1.3 %copy.10 = bf16[8,448]{1,0:T(8,128)(2,1)} copy(bf16[8,448]{1,0:T(8,128)(2,1)} %shard_map.82) | data formatting | bytes 14336

commit v3 on v2

--- a/solution.py
+++ b/solution.py
@@ -24,45 +24,38 @@
 def spread(slots, chips, z, c, send, recv, relay):
     def copy(k):
         there = lax.rem(z + k, chips) * CORES + c
-        return remote(slots.at[c, z], slots.at[c, z], send.at[k], recv.at[k], {"seq": there})
-
-    def start(i, _):
-        far = chips // 2
-        step = (i + 1) // 2
-        k = jnp.where(lax.rem(i, 2) == 0, far - step, far + step)
+        return remote(slots.at[c, z], slots.at[c, z], send, recv.at[k], {"seq": there})
+
+    for k in far_first(chips):
         copy(k).start()
-        return 0
-
-    lax.fori_loop(0, chips - 1, start, 0)
-
-    def arrive(k, _):
+    for k in range(1, chips):
         copy(k).wait_recv()
-        return 0
-
-    lax.fori_loop(1, chips, arrive, 0)
-    half = remote(slots.at[c], slots.at[c], relay.at[0], relay.at[1], {"seq": z * CORES + (1 - c)})
+    partner = {"seq": z * CORES + 1 - c}
+    half = remote(slots.at[c], slots.at[c], relay.at[0], relay.at[1], partner)
     half.start()
     half.wait_recv()
 
     def drain():
-        def sent(k, _):
-            copy(k).wait_send()
-            return 0
-
-        lax.fori_loop(1, chips, sent, 0)
+        every = pl.ds(0, chips - 1)
+        remote(slots.at[c, every], slots.at[c, every], send, relay.at[1], partner).wait_send()
         half.wait_send()
 
     return drain
+
+
+def far_first(n):
+    return sorted(range(1, n), key=lambda m: -min(m, n - m))
 
 
 def kernel(
     chips, owners, heads,
     q_hbm, k_hbm, v_hbm, slopes_hbm, block_seq_hbm, block_pos_hbm, lengths_hbm, w_hbm, out,
     slopes, block_seq, block_pos, lengths, kbuf, vbuf, wbuf, qall, gall, part, landed,
-    load, q_send, q_recv, q_relay, g_send, g_recv, g_relay, p_send, p_recv,
+    load, met, e_send, e_recv, q_send, q_recv, g_send, g_recv, g_relay, p_send, p_recv,
 ):
     seq = lax.axis_index("seq")
     mine = lax.axis_index("tensor")
+    devices = CORES * chips
     z, c = seq // CORES, lax.rem(seq, CORES)
     blocks, block_len, features = k_hbm.shape
     rows = q_hbm.shape[0]
@@ -70,28 +63,34 @@
     seqs = lengths_hbm.shape[0]
     scale = 1.0 / math.sqrt(head_dim)
 
+    near = jnp.minimum(mine, owners - mine)
+    rank = jnp.where(mine * 2 > owners, 2 * near - 1, jnp.where(mine * 2 == owners, owners - 1, 2 * near))
+
+    def owner_of(r):
+        half = (r + 1) // 2
+        return jnp.where(r == owners - 1, owners // 2, jnp.where(lax.rem(r, 2) == 1, owners - half, half))
+
+    place = lax.rem(seq + devices - 1, devices)
+    last = chips - 1
+
     barrier = pltpu.get_barrier_semaphore()
 
-    def greet_chip(k, _):
-        there = lax.rem(z + k, chips) * CORES + c
+    def greet_seq(at, _):
+        there = lax.rem(at + 1, devices)
         pl.semaphore_signal(barrier, inc=1, device_id={"seq": there}, device_id_type=MESH)
         return 0
 
-    def greet_owner(k, _):
-        there = lax.rem(mine + k, owners)
-        pl.semaphore_signal(barrier, inc=1, device_id={"tensor": there}, device_id_type=MESH)
-        return 0
-
-    lax.fori_loop(1, chips, greet_chip, 0)
-    pl.semaphore_signal(
-        barrier, inc=1, device_id={"seq": z * CORES + (1 - c)}, device_id_type=MESH
-    )
-    lax.fori_loop(1, owners, greet_owner, 0)
-
-    q_load = pltpu.make_async_copy(q_hbm, qall.at[c, z], load.at[0])
-    k_load = pltpu.make_async_copy(k_hbm, kbuf, load.at[1])
-    v_load = pltpu.make_async_copy(v_hbm, vbuf, load.at[2])
-    w_load = pltpu.make_async_copy(w_hbm, wbuf, load.at[3])
+    def greet_owner(r, _):
+        pl.semaphore_signal(
+            barrier, inc=1, device_id={"tensor": owner_of(r)}, device_id_type=MESH
+        )
+        return 0
+
+    q_load = pltpu.make_async_copy(q_hbm, qall.at[seq], load.at[0])
+    q_load.start()
+    lax.fori_loop(place + 1, devices, greet_seq, 0)
+    lax.fori_loop(rank + 1, owners, greet_owner, 0)
+
     small = [
         pltpu.make_async_copy(src, dst, load.at[4 + i])
         for i, (src, dst) in enumerate(
@@ -103,16 +102,102 @@
             )
         )
     ]
-    q_load.start()
+    k_load = pltpu.make_async_copy(k_hbm, kbuf, load.at[1])
+    v_load = pltpu.make_async_copy(v_hbm, vbuf, load.at[2])
+    w_load = pltpu.make_async_copy(w_hbm, wbuf, load.at[3])
     for copy in small:
         copy.start()
     k_load.start()
     v_load.start()
     w_load.start()
     q_load.wait()
-    pl.semaphore_wait(barrier, chips - 1 + 1 + owners - 1)
-
-    q_drain = spread(qall, chips, z, c, q_send, q_recv, q_relay)
+
+    @pl.when(place + rank > 0)
+    def _():
+        pl.semaphore_wait(barrier, place + rank)
+
+    def give_q(j):
+        return remote(qall.at[seq], qall.at[seq], q_send, q_recv.at[seq], {"seq": j})
+
+    def arrival(j):
+        return remote(qall.at[j], qall.at[j], q_send, q_recv.at[j], {"seq": z * CORES + 1 - c})
+
+    def send_down(i, _):
+        far = chips // 2
+        step = (i + 1) // 2
+        k = jnp.where(lax.rem(i, 2) == 0, far - step, far + step)
+        for cc in range(CORES):
+            j = lax.rem(z + k, chips) * CORES + cc
+
+            @pl.when(lax.rem(j + devices - 1, devices) < place)
+            def _():
+                give_q(j).start()
+
+        return 0
+
+    lax.fori_loop(0, chips, send_down, 0)
+
+    def hail_owner(r, _):
+        pl.semaphore_signal(met, inc=1, device_id={"tensor": owner_of(r)}, device_id_type=MESH)
+        return 0
+
+    lax.fori_loop(0, rank, hail_owner, 0)
+
+    early = pl.ds(1, (last - 1) * CORES - 1)
+
+    def bulk(j, i):
+        return remote(qall.at[early], qall.at[early], e_send.at[i], e_recv, {"seq": j})
+
+    def send_up(at, _):
+        j = lax.rem(at + 1, devices)
+        arrival(j).wait_recv()
+
+        @pl.when((j // CORES != last) | (z >= last - 1) | (seq == 0))
+        def _():
+            give_q(j).start()
+
+        return 0
+
+    lax.fori_loop(place + 1, devices - CORES - 1, send_up, 0)
+    lax.fori_loop(jnp.maximum(place + 1, devices - CORES - 1), devices - 1, send_up, 0)
+
+    @pl.when(seq == 1)
+    def _():
+        for i in range(CORES):
+            bulk(last * CORES + i, i).start()
+
+    @pl.when(place < devices - 1)
+    def _():
+        send_up(devices - 1, 0)
+
+    def arrive(at, _):
+        arrival(lax.rem(at + 1, devices)).wait_recv()
+        return 0
+
+    @pl.when(z == last)
+    def _():
+        bulk(seq, 0).wait_recv()
+        lax.fori_loop((last - 1) * CORES - 1, place, arrive, 0)
+
+    @pl.when(z != last)
+    def _():
+        lax.fori_loop(0, place, arrive, 0)
+
+    def q_drain():
+        @pl.when((z >= last - 1) | (seq == 0))
+        def _():
+            every = pl.ds(0, devices - 1)
+            remote(qall.at[every], qall.at[every], q_send, e_recv, {"seq": z * CORES + 1 - c}).wait_send()
+
+        @pl.when((z < last - 1) & (seq != 0))
+        def _():
+            every = pl.ds(0, devices - 1 - CORES)
+            remote(qall.at[every], qall.at[every], q_send, e_recv, {"seq": z * CORES + 1 - c}).wait_send()
+
+        @pl.when(seq == 1)
+        def _():
+            for i in range(CORES):
+                bulk(last * CORES + i, i).wait_send()
 
     sub = lax.broadcasted_iota(jnp.int32, (8, features), 0)
     lane = lax.broadcasted_iota(jnp.int32, (8, features), 1)
@@ -135,7 +220,7 @@
         length = lengths[s]
         owner = s // rows
         r = lax.rem(s, rows)
-        pair = qall[lax.rem(owner, CORES), owner // CORES].astype(F32)
+        pair = qall[owner].astype(F32)
         row = pair[0:1]
         for i in range(1, rows):
             row = jnp.where(r == i, pair[i : i + 1], row)
@@ -223,32 +308,24 @@
         there = lax.rem(mine + k, owners)
         return remote(part.at[there], landed.at[k], p_send.at[k], p_recv.at[k], {"tensor": there})
 
-    def give_start(i, _):
-        far = owners // 2
-        step = (i + 1) // 2
-        give(jnp.where(lax.rem(i, 2) == 0, far - step, far + step)).start()
-        return 0
-
-    lax.fori_loop(0, owners - 1, give_start, 0)
+    @pl.when(rank < owners - 1)
+    def _():
+        pl.semaphore_wait(met, owners - 1 - rank)
+
+    for k in far_first(owners):
+        give(k).start()
     result = part[mine].astype(F32)
 
-    def give_arrive(k, _):
+    for k in range(1, owners):
         give(k).wait_recv()
-        return 0
-
-    lax.fori_loop(1, owners, give_arrive, 0)
-    for k in range(1, owners):
         result = result + landed[k].astype(F32)
     out[...] = result.astype(BF16)
 
     q_drain()
     g_drain()
 
-    def give_sent(k, _):
+    for k in range(1, owners):
         give(k).wait_send()
-        return 0
-
-    lax.fori_loop(1, owners, give_sent, 0)
 
 
 def solution(mesh):
@@ -267,7 +344,7 @@
         dma = pltpu.SemaphoreType.DMA
         return pl.pallas_call(
             functools.partial(kernel, chips, owners, heads),
-            out_shape=jax.ShapeDtypeStruct((seqs // owners, columns), BF16),
+            out_shape=pltpu.VMEM((seqs // owners, columns), BF16),
             in_specs=[hbm] * 8,
             out_specs=pl.BlockSpec(memory_space=pltpu.VMEM),
             scratch_shapes=[
@@ -278,15 +355,17 @@
                 pltpu.VMEM(key_cache.shape, BF16),
                 pltpu.VMEM(value_cache.shape, BF16),
                 pltpu.VMEM(out_weight.shape[::-1], BF16),
-                pltpu.VMEM((CORES, chips, rows, features), BF16),
+                pltpu.VMEM((CORES * chips, rows, features), BF16),
                 pltpu.VMEM((CORES, chips, *message), BF16),
                 pltpu.VMEM((owners, seqs // owners, columns), BF16),
                 pltpu.VMEM((owners, seqs // owners, columns), BF16),
                 dma((8,)),
-                dma((chips,)),
-                dma((chips,)),
-                dma((2,)),
-                dma((chips,)),
+                pltpu.SemaphoreType.REGULAR,
+                dma((CORES,)),
+                dma,
+                dma,
+                dma((CORES * chips,)),
+                dma,
                 dma((chips,)),
                 dma((2,)),
                 dma((owners,)),

time: 78.3 us -> 75 us (0.958)
  Pallas kernels: 76.3 us -> 74.3 us
    pallas_call x1, Pallas kernels: 76.3 us -> 74.3 us  [local(): pl.pallas_call(functools.partial(kernel, chips, owners, heads), out_shape...]
where the time goes in v3:
time: 75 us; the launch traced here: 74.9 us
  Pallas kernels  74.3 us (99%)
    pallas_call x1, Pallas kernels, local(): pl.pallas_call(functools.partial(kernel, chips, owners, heads), out_shape...  74.3 us

profile of v3, /device:TPU:65, one launch (start us, length us, event | category | flops | bytes accessed | tf_op | source)
XLA Modules:
  0.0 74.9 jit_solution(17283099354326693193)
XLA Ops:
  0.0 74.3 %shard_map.82 = bf16[8,448]{1,0:T(8,128)(2,1)S(1)} custom-call(bf16[2,896]{1,0:T(2,128)(2,1)} %q_hbm.1, bf16[4,256,896]{2,1,0:T(8,128)(2,1)} %k_hbm.1, bf16[4,256,896]{2,1,0:T(8,128)(2,1)} %v_hbm.1, f32[7]{0:T(128)} %slopes_hbm.1, s32[4]{0:T(128)} %block_seq_hbm.1, s32[4]{0:T(128)} %block_pos_hbm.1, s32[64]{0:T(128)} %lengths_hbm.1, bf16[448,896]{1,0:T(8,128)(2,1)} %bitcast.1), custom_call_target="tpu_custom_call" | custom-call | tf_op jit(solution)/shard_map/pallas_call | solution.py:345
  74.3 0.6 copy.10

commit v4 on v3

--- a/solution.py
+++ b/solution.py
@@ -50,8 +50,8 @@
 def kernel(
     chips, owners, heads,
     q_hbm, k_hbm, v_hbm, slopes_hbm, block_seq_hbm, block_pos_hbm, lengths_hbm, w_hbm, out,
-    slopes, block_seq, block_pos, lengths, kbuf, vbuf, wbuf, qall, gall, part, landed,
-    load, met, e_send, e_recv, q_send, q_recv, g_send, g_recv, g_relay, p_send, p_recv,
+    slopes, block_seq, block_pos, lengths, kbuf, kturn, vbuf, wbuf, qall, gall, part, landed,
+    load, met, f_send, f_recv, e_recv, r_recv, q_send, q_recv, g_send, g_recv, g_relay, p_send, p_recv,
 ):
     seq = lax.axis_index("seq")
     mine = lax.axis_index("tensor")
@@ -70,14 +70,12 @@
         half = (r + 1) // 2
         return jnp.where(r == owners - 1, owners // 2, jnp.where(lax.rem(r, 2) == 1, owners - half, half))
 
-    place = lax.rem(seq + devices - 1, devices)
     last = chips - 1
 
     barrier = pltpu.get_barrier_semaphore()
 
-    def greet_seq(at, _):
-        there = lax.rem(at + 1, devices)
-        pl.semaphore_signal(barrier, inc=1, device_id={"seq": there}, device_id_type=MESH)
+    def greet_seq(j, _):
+        pl.semaphore_signal(barrier, inc=1, device_id={"seq": j}, device_id_type=MESH)
         return 0
 
     def greet_owner(r, _):
@@ -88,7 +86,15 @@
 
     q_load = pltpu.make_async_copy(q_hbm, qall.at[seq], load.at[0])
     q_load.start()
-    lax.fori_loop(place + 1, devices, greet_seq, 0)
+
+    @pl.when(seq > 0)
+    def _():
+        lax.fori_loop(seq + 1, devices, greet_seq, 0)
+
+    @pl.when(seq == 1)
+    def _():
+        greet_seq(0, 0)
+
     lax.fori_loop(rank + 1, owners, greet_owner, 0)
 
     small = [
@@ -111,16 +117,24 @@
     v_load.start()
     w_load.start()
     q_load.wait()
-
-    @pl.when(place + rank > 0)
-    def _():
-        pl.semaphore_wait(barrier, place + rank)
+    before = jnp.where(seq == 0, 1, seq - 1) + rank
+
+    @pl.when(before > 0)
+    def _():
+        pl.semaphore_wait(barrier, before)
 
     def give_q(j):
         return remote(qall.at[seq], qall.at[seq], q_send, q_recv.at[seq], {"seq": j})
 
     def arrival(j):
         return remote(qall.at[j], qall.at[j], q_send, q_recv.at[j], {"seq": z * CORES + 1 - c})
+
+    def several(slots, recv, j, send=q_send):
+        return remote(qall.at[slots], qall.at[slots], send, recv, {"seq": j})
+
+    pair = pl.ds(0, CORES)
+    rest = pl.ds(1, devices - 1)
+    early = pl.ds(0, (last - 1) * CORES)
 
     def send_down(i, _):
         far = chips // 2
@@ -129,7 +143,7 @@
         for cc in range(CORES):
             j = lax.rem(z + k, chips) * CORES + cc
 
-            @pl.when(lax.rem(j + devices - 1, devices) < place)
+            @pl.when((j > 0) & (j < seq))
             def _():
                 give_q(j).start()
 
@@ -143,61 +157,81 @@
 
     lax.fori_loop(0, rank, hail_owner, 0)
 
-    early = pl.ds(1, (last - 1) * CORES - 1)
-
-    def bulk(j, i):
-        return remote(qall.at[early], qall.at[early], e_send.at[i], e_recv, {"seq": j})
-
-    def send_up(at, _):
-        j = lax.rem(at + 1, devices)
+    k_load.wait()
+    for b in range(blocks):
+        kturn[b] = kbuf[b].T
+
+    def arrive(j, _):
         arrival(j).wait_recv()
-
-        @pl.when((j // CORES != last) | (z >= last - 1) | (seq == 0))
-        def _():
-            give_q(j).start()
-
         return 0
 
-    lax.fori_loop(place + 1, devices - CORES - 1, send_up, 0)
-    lax.fori_loop(jnp.maximum(place + 1, devices - CORES - 1), devices - 1, send_up, 0)
+    @pl.when(seq == 0)
+    def _():
+        give_q(1).start()
+        several(rest, r_recv, 1).wait_recv()
 
     @pl.when(seq == 1)
     def _():
-        for i in range(CORES):
-            bulk(last * CORES + i, i).start()
-
-    @pl.when(place < devices - 1)
-    def _():
-        send_up(devices - 1, 0)
-
-    def arrive(at, _):
-        arrival(lax.rem(at + 1, devices)).wait_recv()
-        return 0
-
-    @pl.when(z == last)
-    def _():
-        bulk(seq, 0).wait_recv()
-        lax.fori_loop((last - 1) * CORES - 1, place, arrive, 0)
-
-    @pl.when(z != last)
-    def _():
-        lax.fori_loop(0, place, arrive, 0)
+        arrival(0).wait_recv()
+
+        def pass_pair(j, _):
+            arrival(j).wait_recv()
+            several(pair, f_recv, j, f_send).start()
+            return 0
+
+        lax.fori_loop(CORES, last * CORES, pass_pair, 0)
+
+        def pass_early(j, _):
+            arrival(j).wait_recv()
+            several(early, e_recv, j, f_send).start()
+            return 0
+
+        lax.fori_loop(last * CORES, devices, pass_early, 0)
+        several(rest, r_recv, 0).start()
+
+    @pl.when(seq > 1)
+    def _():
+        def send_up(j, _):
+            arrival(j).wait_recv()
+
+            @pl.when((j // CORES != last) | (z >= last - 1))
+            def _():
+                give_q(j).start()
+
+            return 0
+
+        lax.fori_loop(seq + 1, devices, send_up, 0)
+
+        @pl.when(z == last)
+        def _():
+            several(early, e_recv, 1).wait_recv()
+            lax.fori_loop((last - 1) * CORES, seq, arrive, 0)
+
+        @pl.when(z != last)
+        def _():
+            several(pair, f_recv, 1).wait_recv()
+            lax.fori_loop(CORES, seq, arrive, 0)
 
     def q_drain():
-        @pl.when((z >= last - 1) | (seq == 0))
-        def _():
-            every = pl.ds(0, devices - 1)
-            remote(qall.at[every], qall.at[every], q_send, e_recv, {"seq": z * CORES + 1 - c}).wait_send()
-
-        @pl.when((z < last - 1) & (seq != 0))
-        def _():
-            every = pl.ds(0, devices - 1 - CORES)
-            remote(qall.at[every], qall.at[every], q_send, e_recv, {"seq": z * CORES + 1 - c}).wait_send()
+        far = (last - 1) * CORES
+
+        @pl.when(seq == 0)
+        def _():
+            give_q(1).wait_send()
 
         @pl.when(seq == 1)
         def _():
-            for i in range(CORES):
-                bulk(last * CORES + i, i).wait_send()
+            several(rest, r_recv, 0).wait_send()
+            size = kbuf.at[0, pl.ds(0, 2 * CORES * far * rows)]
+            remote(size, size, f_send, r_recv, {"seq": 0}).wait_send()
+
+        @pl.when((seq > 1) & (z < last - 1))
+        def _():
+            several(pl.ds(0, devices - 2 - CORES), r_recv, 1).wait_send()
+
+        @pl.when(z >= last - 1)
+        def _():
+            several(pl.ds(0, devices - 2), r_recv, 1).wait_send()
 
     sub = lax.broadcasted_iota(jnp.int32, (8, features), 0)
     lane = lax.broadcasted_iota(jnp.int32, (8, features), 1)
@@ -207,7 +241,6 @@
     a_sub = lax.broadcasted_iota(jnp.int32, (8, head_dim), 0)
     a_lane = lax.broadcasted_iota(jnp.int32, (8, head_dim), 1)
 
-    k_load.wait()
     v_load.wait()
     for copy in small:
         copy.wait()
@@ -226,7 +259,7 @@
             row = jnp.where(r == i, pair[i : i + 1], row)
         wide = jnp.where(own_head, jnp.broadcast_to(row, (8, features)), 0.0).astype(BF16)
         scores = lax.dot_general(
-            wide, kbuf[b], (((1,), (1,)), ((), ())), preferred_element_type=F32
+            wide, kturn[b], (((1,), (0,)), ((), ())), preferred_element_type=F32
         )
         placed = block_pos[b] * block_len + t_at
         live = placed < length
@@ -353,6 +386,7 @@
                 pltpu.SMEM(block_pos.shape, jnp.int32),
                 pltpu.SMEM(lengths.shape, jnp.int32),
                 pltpu.VMEM(key_cache.shape, BF16),
+                pltpu.VMEM((blocks, features, block_len), BF16),
                 pltpu.VMEM(value_cache.shape, BF16),
                 pltpu.VMEM(out_weight.shape[::-1], BF16),
                 pltpu.VMEM((CORES * chips, rows, features), BF16),
@@ -361,7 +395,9 @@
                 pltpu.VMEM((owners, seqs // owners, columns), BF16),
                 dma((8,)),
                 pltpu.SemaphoreType.REGULAR,
-                dma((CORES,)),
+                dma,
+                dma,
+                dma,
                 dma,
                 dma,
                 dma((CORES * chips,)),

time: 75 us -> 73.3 us (0.977)
  Pallas kernels: 74.3 us -> 72.5 us
    pallas_call x1, Pallas kernels: 74.3 us -> 72.5 us  [local(): pl.pallas_call(functools.partial(kernel, chips, owners, heads), out_shape...]
where the time goes in v4:
time: 73.3 us; the launch traced here: 73.2 us
  Pallas kernels  72.5 us (99%)
    pallas_call x1, Pallas kernels, local(): pl.pallas_call(functools.partial(kernel, chips, owners, heads), out_shape...  72.5 us

profile of v4, /device:TPU:65, one launch (start us, length us, event | category | flops | bytes accessed | tf_op | source)
XLA Modules:
  0.0 73.2 jit_solution(8402825110978896989)
XLA Ops:
  0.0 72.5 %shard_map.82 = bf16[8,448]{1,0:T(8,128)(2,1)S(1)} custom-call(bf16[2,896]{1,0:T(2,128)(2,1)} %q_hbm.1, bf16[4,256,896]{2,1,0:T(8,128)(2,1)} %k_hbm.1, bf16[4,256,896]{2,1,0:T(8,128)(2,1)} %v_hbm.1, f32[7]{0:T(128)} %slopes_hbm.1, s32[4]{0:T(128)} %block_seq_hbm.1, s32[4]{0:T(128)} %block_pos_hbm.1, s32[64]{0:T(128)} %lengths_hbm.1, bf16[448,896]{1,0:T(8,128)(2,1)} %bitcast.1), custom_call_target="tpu_custom_call" | custom-call | tf_op jit(solution)/shard_map/pallas_call | solution.py:378
  72.5 0.6 copy.10

commit v5 on v4

--- a/solution.py
+++ b/solution.py
@@ -12,6 +12,8 @@
 F32 = jnp.float32
 BF16 = jnp.bfloat16
 CORES = 2
+HUBS = (3, -3, 6, -6)
+LATE = 3
 GONE = -1e30
 
 
@@ -22,23 +24,33 @@
 
 
 def spread(slots, chips, z, c, send, recv, relay):
-    def copy(k):
-        there = lax.rem(z + k, chips) * CORES + c
-        return remote(slots.at[c, z], slots.at[c, z], send, recv.at[k], {"seq": there})
-
-    for k in far_first(chips):
-        copy(k).start()
-    for k in range(1, chips):
-        copy(k).wait_recv()
     partner = {"seq": z * CORES + 1 - c}
+
+    def pass_on(place, step):
+        there = lax.rem(z + chips + step, chips) * CORES + c
+        at = (place + step) % chips
+        sem = recv.at[HUBS.index(step)] if place == 0 and step in HUBS else recv.at[len(HUBS)]
+        remote(slots.at[c, place % chips], slots.at[c, at], send, sem, {"seq": there}).start()
+
+    def landed(at, sem):
+        remote(slots.at[c, at], slots.at[c, at], send, sem, partner).wait_recv()
+
+    direct = [step for step in range(-(chips // 2) + 1, chips // 2 + 1) if step in HUBS or abs(step) in (1, chips // 2)]
+    for step in sorted(direct, key=lambda step: -abs(step)):
+        pass_on(0, step)
+    for i, hub in enumerate(HUBS):
+        landed(hub % chips, recv.at[i])
+        for step in (1, -1):
+            pass_on(hub, step)
+    landed(pl.ds(0, chips - 1 - len(HUBS)), recv.at[len(HUBS)])
     half = remote(slots.at[c], slots.at[c], relay.at[0], relay.at[1], partner)
     half.start()
     half.wait_recv()
 
     def drain():
+        half.wait_send()
         every = pl.ds(0, chips - 1)
         remote(slots.at[c, every], slots.at[c, every], send, relay.at[1], partner).wait_send()
-        half.wait_send()
 
     return drain
 
@@ -51,7 +63,7 @@
     chips, owners, heads,
     q_hbm, k_hbm, v_hbm, slopes_hbm, block_seq_hbm, block_pos_hbm, lengths_hbm, w_hbm, out,
     slopes, block_seq, block_pos, lengths, kbuf, kturn, vbuf, wbuf, qall, gall, part, landed,
-    load, met, f_send, f_recv, e_recv, r_recv, q_send, q_recv, g_send, g_recv, g_relay, p_send, p_recv,
+    load, met, e_send, f_send, f_recv, e_recv, r_recv, d_recv, q_send, q_recv, g_send, g_recv, g_relay, p_send, p_recv,
 ):
     seq = lax.axis_index("seq")
     mine = lax.axis_index("tensor")
@@ -63,14 +75,11 @@
     seqs = lengths_hbm.shape[0]
     scale = 1.0 / math.sqrt(head_dim)
 
-    near = jnp.minimum(mine, owners - mine)
-    rank = jnp.where(mine * 2 > owners, 2 * near - 1, jnp.where(mine * 2 == owners, owners - 1, 2 * near))
-
-    def owner_of(r):
-        half = (r + 1) // 2
-        return jnp.where(r == owners - 1, owners // 2, jnp.where(lax.rem(r, 2) == 1, owners - half, half))
-
-    last = chips - 1
+    order = sorted(range(owners), key=lambda x: (min(x, owners - x), x * 2 <= owners))
+    order = order[:-3] + [owners // 2] + [x for x in order[-3:] if x * 2 != owners]
+    rank = sum(jnp.where(mine == x, r, 0) for r, x in enumerate(order))
+
+    first_late = chips - LATE
 
     barrier = pltpu.get_barrier_semaphore()
 
@@ -78,12 +87,6 @@
         pl.semaphore_signal(barrier, inc=1, device_id={"seq": j}, device_id_type=MESH)
         return 0
 
-    def greet_owner(r, _):
-        pl.semaphore_signal(
-            barrier, inc=1, device_id={"tensor": owner_of(r)}, device_id_type=MESH
-        )
-        return 0
-
     q_load = pltpu.make_async_copy(q_hbm, qall.at[seq], load.at[0])
     q_load.start()
 
@@ -95,7 +98,12 @@
     def _():
         greet_seq(0, 0)
 
-    lax.fori_loop(rank + 1, owners, greet_owner, 0)
+    for r, x in enumerate(order):
+
+        @pl.when(r > rank)
+        def _(x=x):
+            pl.semaphore_signal(barrier, inc=1, device_id={"tensor": x}, device_id_type=MESH)
+
 
     small = [
         pltpu.make_async_copy(src, dst, load.at[4 + i])
@@ -134,7 +142,9 @@
 
     pair = pl.ds(0, CORES)
     rest = pl.ds(1, devices - 1)
-    early = pl.ds(0, (last - 1) * CORES)
+
+    def early(core):
+        return pl.ds(core * first_late, first_late)
 
     def send_down(i, _):
         far = chips // 2
@@ -151,11 +161,11 @@
 
     lax.fori_loop(0, chips, send_down, 0)
 
-    def hail_owner(r, _):
-        pl.semaphore_signal(met, inc=1, device_id={"tensor": owner_of(r)}, device_id_type=MESH)
-        return 0
-
-    lax.fori_loop(0, rank, hail_owner, 0)
+    for r, x in enumerate(order):
+
+        @pl.when(r < rank)
+        def _(x=x):
+            pl.semaphore_signal(met, inc=1, device_id={"tensor": x}, device_id_type=MESH)
 
     k_load.wait()
     for b in range(blocks):
@@ -179,14 +189,14 @@
             several(pair, f_recv, j, f_send).start()
             return 0
 
-        lax.fori_loop(CORES, last * CORES, pass_pair, 0)
+        lax.fori_loop(CORES, first_late * CORES, pass_pair, 0)
 
         def pass_early(j, _):
             arrival(j).wait_recv()
-            several(early, e_recv, j, f_send).start()
+            several(early(lax.rem(j, CORES)), e_recv, j, e_send.at[j - first_late * CORES]).start()
             return 0
 
-        lax.fori_loop(last * CORES, devices, pass_early, 0)
+        lax.fori_loop(first_late * CORES, devices, pass_early, 0)
         several(rest, r_recv, 0).start()
 
     @pl.when(seq > 1)
@@ -194,7 +204,7 @@
         def send_up(j, _):
             arrival(j).wait_recv()
 
-            @pl.when((j // CORES != last) | (z >= last - 1))
+            @pl.when((j < first_late * CORES) | (z >= first_late))
             def _():
                 give_q(j).start()
 
@@ -202,19 +212,19 @@
 
         lax.fori_loop(seq + 1, devices, send_up, 0)
 
-        @pl.when(z == last)
-        def _():
-            several(early, e_recv, 1).wait_recv()
-            lax.fori_loop((last - 1) * CORES, seq, arrive, 0)
-
-        @pl.when(z != last)
+        @pl.when(z >= first_late)
+        def _():
+            several(early(c), e_recv, 1).wait_recv()
+            several(early(c), d_recv, z * CORES + 1 - c, f_send).start()
+            lax.fori_loop(first_late * CORES, seq, arrive, 0)
+            several(early(1 - c), d_recv, 1).wait_recv()
+
+        @pl.when(z < first_late)
         def _():
             several(pair, f_recv, 1).wait_recv()
             lax.fori_loop(CORES, seq, arrive, 0)
 
     def q_drain():
-        far = (last - 1) * CORES
-
         @pl.when(seq == 0)
         def _():
             give_q(1).wait_send()
@@ -222,16 +232,19 @@
         @pl.when(seq == 1)
         def _():
             several(rest, r_recv, 0).wait_send()
-            size = kbuf.at[0, pl.ds(0, 2 * CORES * far * rows)]
+            size = kbuf.at[0, pl.ds(0, (first_late - 1) * CORES * CORES * rows)]
             remote(size, size, f_send, r_recv, {"seq": 0}).wait_send()
-
-        @pl.when((seq > 1) & (z < last - 1))
-        def _():
-            several(pl.ds(0, devices - 2 - CORES), r_recv, 1).wait_send()
-
-        @pl.when(z >= last - 1)
+            for i in range(LATE * CORES):
+                several(early(0), e_recv, 0, e_send.at[i]).wait_send()
+
+        @pl.when((seq > 1) & (z < first_late))
+        def _():
+            several(pl.ds(0, devices - 2 - LATE * CORES), r_recv, 1).wait_send()
+
+        @pl.when(z >= first_late)
         def _():
             several(pl.ds(0, devices - 2), r_recv, 1).wait_send()
+            several(early(c), r_recv, 1, f_send).wait_send()
 
     sub = lax.broadcasted_iota(jnp.int32, (8, features), 0)
     lane = lax.broadcasted_iota(jnp.int32, (8, features), 1)
@@ -292,7 +305,7 @@
             piece = wholes[b][:, j * wide : (j + 1) * wide]
             half = jnp.where(m_sub == i, jnp.broadcast_to(piece, (8, wide)), half)
         halves.append(half)
-    gall[c, z] = jnp.concatenate(halves, axis=0).astype(BF16)
+    gall[c, 0] = jnp.concatenate(halves, axis=0).astype(BF16)
 
     g_drain = spread(gall, chips, z, c, g_send, g_recv, g_relay)
 
@@ -339,7 +352,7 @@
 
     def give(k):
         there = lax.rem(mine + k, owners)
-        return remote(part.at[there], landed.at[k], p_send.at[k], p_recv.at[k], {"tensor": there})
+        return remote(part.at[there], landed.at[k - 1], p_send, p_recv, {"tensor": there})
 
     @pl.when(rank < owners - 1)
     def _():
@@ -349,16 +362,17 @@
         give(k).start()
     result = part[mine].astype(F32)
 
+    others = pl.ds(0, owners - 1)
+    all_others = remote(part.at[others], landed.at[others], p_send, p_recv, {"tensor": mine})
+    all_others.wait_recv()
     for k in range(1, owners):
-        give(k).wait_recv()
-        result = result + landed[k].astype(F32)
+        result = result + landed[k - 1].astype(F32)
     out[...] = result.astype(BF16)
 
     q_drain()
     g_drain()
 
-    for k in range(1, owners):
-        give(k).wait_send()
+    all_others.wait_send()
 
 
 def solution(mesh):
@@ -395,6 +409,8 @@
                 pltpu.VMEM((owners, seqs // owners, columns), BF16),
                 dma((8,)),
                 pltpu.SemaphoreType.REGULAR,
+                dma((LATE * CORES,)),
+                dma,
                 dma,
                 dma,
                 dma,
@@ -402,10 +418,10 @@
                 dma,
                 dma((CORES * chips,)),
                 dma,
-                dma((chips,)),
+                dma((len(HUBS) + 1,)),
                 dma((2,)),
-                dma((owners,)),
-                dma((owners,)),
+                dma,
+                dma,
             ],
             compiler_params=pltpu.CompilerParams(
                 collective_id=0, has_side_effects=True

time: 73.3 us -> 71.8 us (0.980)
  Pallas kernels: 72.5 us -> 71 us
    pallas_call x1, Pallas kernels: 72.5 us -> 71 us  [local(): pl.pallas_call(functools.partial(kernel, chips, owners, heads), out_shape...]
where the time goes in v5:
time: 71.8 us; the launch traced here: 71.6 us
  Pallas kernels  71 us (99%)
    pallas_call x1, Pallas kernels, local(): pl.pallas_call(functools.partial(kernel, chips, owners, heads), out_shape...  71 us

profile of v5, /device:TPU:65, one launch (start us, length us, event | category | flops | bytes accessed | tf_op | source)
XLA Modules:
  0.0 71.6 jit_solution(10719473865234859899)
XLA Ops:
  0.0 71.0 %shard_map.82 = bf16[8,448]{1,0:T(8,128)(2,1)S(1)} custom-call(bf16[2,896]{1,0:T(2,128)(2,1)} %q_hbm.1, bf16[4,256,896]{2,1,0:T(8,128)(2,1)} %k_hbm.1, bf16[4,256,896]{2,1,0:T(8,128)(2,1)} %v_hbm.1, f32[7]{0:T(128)} %slopes_hbm.1, s32[4]{0:T(128)} %block_seq_hbm.1, s32[4]{0:T(128)} %block_pos_hbm.1, s32[64]{0:T(128)} %lengths_hbm.1, bf16[448,896]{1,0:T(8,128)(2,1)} %bitcast.1), custom_call_target="tpu_custom_call" | custom-call | tf_op jit(solution)/shard_map/pallas_call | solution.py:392
  71.0 0.6 copy.10

commit v6 on v5

--- a/solution.py
+++ b/solution.py
@@ -12,7 +12,6 @@
 F32 = jnp.float32
 BF16 = jnp.bfloat16
 CORES = 2
-HUBS = (3, -3, 6, -6)
 LATE = 3
 GONE = -1e30
 
@@ -25,31 +24,17 @@
 
 def spread(slots, chips, z, c, send, recv, relay):
     partner = {"seq": z * CORES + 1 - c}
-
-    def pass_on(place, step):
-        there = lax.rem(z + chips + step, chips) * CORES + c
-        at = (place + step) % chips
-        sem = recv.at[HUBS.index(step)] if place == 0 and step in HUBS else recv.at[len(HUBS)]
-        remote(slots.at[c, place % chips], slots.at[c, at], send, sem, {"seq": there}).start()
-
-    def landed(at, sem):
-        remote(slots.at[c, at], slots.at[c, at], send, sem, partner).wait_recv()
-
-    direct = [step for step in range(-(chips // 2) + 1, chips // 2 + 1) if step in HUBS or abs(step) in (1, chips // 2)]
-    for step in sorted(direct, key=lambda step: -abs(step)):
-        pass_on(0, step)
-    for i, hub in enumerate(HUBS):
-        landed(hub % chips, recv.at[i])
-        for step in (1, -1):
-            pass_on(hub, step)
-    landed(pl.ds(0, chips - 1 - len(HUBS)), recv.at[len(HUBS)])
+    for k in far_first(chips):
+        there = lax.rem(z + k, chips) * CORES + c
+        remote(slots.at[c, 0], slots.at[c, k], send, recv.at[0], {"seq": there}).start()
+    every = pl.ds(0, chips - 1)
+    remote(slots.at[c, every], slots.at[c, every], send, recv.at[0], partner).wait_recv()
     half = remote(slots.at[c], slots.at[c], relay.at[0], relay.at[1], partner)
     half.start()
     half.wait_recv()
 
     def drain():
         half.wait_send()
-        every = pl.ds(0, chips - 1)
         remote(slots.at[c, every], slots.at[c, every], send, relay.at[1], partner).wait_send()
 
     return drain
@@ -63,7 +48,7 @@
     chips, owners, heads,
     q_hbm, k_hbm, v_hbm, slopes_hbm, block_seq_hbm, block_pos_hbm, lengths_hbm, w_hbm, out,
     slopes, block_seq, block_pos, lengths, kbuf, kturn, vbuf, wbuf, qall, gall, part, landed,
-    load, met, e_send, f_send, f_recv, e_recv, r_recv, d_recv, q_send, q_recv, g_send, g_recv, g_relay, p_send, p_recv,
+    load, met, ready, e_send, f_send, f_recv, e_recv, r_recv, d_recv, q_send, q_recv, g_send, g_recv, g_relay, p_send, p_recv,
 ):
     seq = lax.axis_index("seq")
     mine = lax.axis_index("tensor")
@@ -100,7 +85,7 @@
 
     for r, x in enumerate(order):
 
-        @pl.when(r > rank)
+        @pl.when((r > rank) & (seq == 1))
         def _(x=x):
             pl.semaphore_signal(barrier, inc=1, device_id={"tensor": x}, device_id_type=MESH)
 
@@ -125,7 +110,7 @@
     v_load.start()
     w_load.start()
     q_load.wait()
-    before = jnp.where(seq == 0, 1, seq - 1) + rank
+    before = jnp.where(seq == 0, 1, jnp.where(seq == 1, rank, seq - 1))
 
     @pl.when(before > 0)
     def _():
@@ -163,7 +148,7 @@
 
     for r, x in enumerate(order):
 
-        @pl.when(r < rank)
+        @pl.when((r < rank) & (seq == 1))
         def _(x=x):
             pl.semaphore_signal(met, inc=1, device_id={"tensor": x}, device_id_type=MESH)
 
@@ -198,6 +183,15 @@
 
         lax.fori_loop(first_late * CORES, devices, pass_early, 0)
         several(rest, r_recv, 0).start()
+
+        @pl.when(rank < owners - 1)
+        def _():
+            pl.semaphore_wait(met, owners - 1 - rank)
+
+        for step in range(1, owners):
+            there = {"tensor": lax.rem(mine + step, owners)}
+            pl.semaphore_signal(ready, inc=1, device_id=there, device_id_type=MESH)
+
 
     @pl.when(seq > 1)
     def _():
@@ -307,6 +301,10 @@
         halves.append(half)
     gall[c, 0] = jnp.concatenate(halves, axis=0).astype(BF16)
 
+    @pl.when(seq == 1)
+    def _():
+        pl.semaphore_wait(ready, owners - 1)
+
     g_drain = spread(gall, chips, z, c, g_send, g_recv, g_relay)
 
     high_rows = groups * blocks
@@ -353,10 +351,6 @@
     def give(k):
         there = lax.rem(mine + k, owners)
         return remote(part.at[there], landed.at[k - 1], p_send, p_recv, {"tensor": there})
-
-    @pl.when(rank < owners - 1)
-    def _():
-        pl.semaphore_wait(met, owners - 1 - rank)
 
     for k in far_first(owners):
         give(k).start()
@@ -409,6 +403,7 @@
                 pltpu.VMEM((owners, seqs // owners, columns), BF16),
                 dma((8,)),
                 pltpu.SemaphoreType.REGULAR,
+                pltpu.SemaphoreType.REGULAR,
                 dma((LATE * CORES,)),
                 dma,
                 dma,
@@ -418,7 +413,7 @@
                 dma,
                 dma((CORES * chips,)),
                 dma,
-                dma((len(HUBS) + 1,)),
+                dma((1,)),
                 dma((2,)),
                 dma,
                 dma,

time: 71.8 us -> 70.6 us (0.983)
  Pallas kernels: 71 us -> 69.9 us
    pallas_call x1, Pallas kernels: 71 us -> 69.9 us  [local(): pl.pallas_call(functools.partial(kernel, chips, owners, heads), out_shape...]
where the time goes in v6:
time: 70.6 us; the launch traced here: 70.5 us
  Pallas kernels  69.9 us (99%)
    pallas_call x1, Pallas kernels, local(): pl.pallas_call(functools.partial(kernel, chips, owners, heads), out_shape...  69.9 us

profile of v6, /device:TPU:65, one launch (start us, length us, event | category | flops | bytes accessed | tf_op | source)
XLA Modules:
  0.0 70.5 jit_solution(8527806099295188037)
XLA Ops:
  0.0 69.9 %shard_map.82 = bf16[8,448]{1,0:T(8,128)(2,1)S(1)} custom-call(bf16[2,896]{1,0:T(2,128)(2,1)} %q_hbm.1, bf16[4,256,896]{2,1,0:T(8,128)(2,1)} %k_hbm.1, bf16[4,256,896]{2,1,0:T(8,128)(2,1)} %v_hbm.1, f32[7]{0:T(128)} %slopes_hbm.1, s32[4]{0:T(128)} %block_seq_hbm.1, s32[4]{0:T(128)} %block_pos_hbm.1, s32[64]{0:T(128)} %lengths_hbm.1, bf16[448,896]{1,0:T(8,128)(2,1)} %bitcast.1), custom_call_target="tpu_custom_call" | custom-call | tf_op jit(solution)/shard_map/pallas_call | solution.py:386
  69.9 0.6 copy.10

commit v7 on v6

--- a/solution.py
+++ b/solution.py
@@ -24,9 +24,14 @@
 
 def spread(slots, chips, z, c, send, recv, relay):
     partner = {"seq": z * CORES + 1 - c}
-    for k in far_first(chips):
-        there = lax.rem(z + k, chips) * CORES + c
-        remote(slots.at[c, 0], slots.at[c, k], send, recv.at[0], {"seq": there}).start()
+    for chip in range(chips):
+
+        @pl.when(chip != z)
+        def _():
+            behind = lax.rem(chip - z + chips, chips)
+            there = {"seq": chip * CORES + c}
+            remote(slots.at[c, 0], slots.at[c, behind], send, recv.at[0], there).start()
+
     every = pl.ds(0, chips - 1)
     remote(slots.at[c, every], slots.at[c, every], send, recv.at[0], partner).wait_recv()
     half = remote(slots.at[c], slots.at[c], relay.at[0], relay.at[1], partner)

time: 70.6 us -> 69.2 us (0.980)
  Pallas kernels: 69.9 us -> 68.4 us
    pallas_call x1, Pallas kernels: 69.9 us -> 68.4 us  [local(): pl.pallas_call(functools.partial(kernel, chips, owners, heads), out_shape...]
where the time goes in v7:
time: 69.2 us; the launch traced here: 69.1 us
  Pallas kernels  68.4 us (99%)
    pallas_call x1, Pallas kernels, local(): pl.pallas_call(functools.partial(kernel, chips, owners, heads), out_shape...  68.4 us

profile of v7, /device:TPU:65, one launch (start us, length us, event | category | flops | bytes accessed | tf_op | source)
XLA Modules:
  0.0 69.1 jit_solution(13154031860006162625)
XLA Ops:
  0.0 68.4 %shard_map.82 = bf16[8,448]{1,0:T(8,128)(2,1)S(1)} custom-call(bf16[2,896]{1,0:T(2,128)(2,1)} %q_hbm.1, bf16[4,256,896]{2,1,0:T(8,128)(2,1)} %k_hbm.1, bf16[4,256,896]{2,1,0:T(8,128)(2,1)} %v_hbm.1, f32[7]{0:T(128)} %slopes_hbm.1, s32[4]{0:T(128)} %block_seq_hbm.1, s32[4]{0:T(128)} %block_pos_hbm.1, s32[64]{0:T(128)} %lengths_hbm.1, bf16[448,896]{1,0:T(8,128)(2,1)} %bitcast.1), custom_call_target="tpu_custom_call" | custom-call | tf_op jit(solution)/shard_map/pallas_call | solution.py:391
  68.5 0.6 copy.10

commit v8 on v7

--- a/solution.py
+++ b/solution.py
@@ -281,7 +281,7 @@
         weights = jnp.where(live, jnp.exp(scores - top), 0.0)
         total = jnp.sum(weights, axis=1, keepdims=True)
         acc = jnp.dot(weights.astype(BF16), vbuf[b], preferred_element_type=F32)
-        o = jnp.sum(jnp.where(own_head, acc / total, 0.0), axis=0, keepdims=True)
+        o = jnp.sum(jnp.where(own_head, acc * (1.0 / total), 0.0), axis=0, keepdims=True)
         lse = top + jnp.log(total)
         high = lse.astype(BF16).astype(F32)
         mid = (lse - high).astype(BF16).astype(F32)
@@ -326,7 +326,7 @@
     column = lax.broadcasted_iota(jnp.int32, (seqs, count), 1)
     group_of = lax.rem(column // blocks, groups)
     seq_at = lax.broadcasted_iota(jnp.int32, (seqs, count), 0).astype(F32)
-    shares = []
+    shares, inverse = [], []
     for j in range(groups):
         back = (groups - 1 - j) * blocks
         moved = tails if back == 0 else pltpu.roll(tails, count - back, 1)
@@ -335,12 +335,14 @@
             level = jnp.where(mask, jnp.broadcast_to(moved[h : h + 1], (seqs, count)), GONE)
             best = jnp.max(level, axis=1, keepdims=True)
             share = jnp.exp(level - best)
-            share = share / jnp.sum(share, axis=1, keepdims=True)
+            inverse.append(1.0 / jnp.sum(share, axis=1, keepdims=True))
             shares.append(share.astype(BF16))
     mixed = jnp.dot(jnp.concatenate(shares, axis=0), both, preferred_element_type=F32)
     attention = jnp.concatenate(
         [
-            mixed[h * seqs : (h + 1) * seqs, (h % 2) * head_dim : (h % 2 + 1) * head_dim].astype(BF16)
+            (
+                mixed[h * seqs : (h + 1) * seqs, (h % 2) * head_dim : (h % 2 + 1) * head_dim] * inverse[h]
+            ).astype(BF16)
             for h in range(heads)
         ],
         axis=1,

time: 69.2 us -> 69.1 us (level)
  no operation moved by 1% of the time
where the time goes in v8:
time: 69.1 us; the launch traced here: 68.9 us
  Pallas kernels  68.3 us (99%)
    pallas_call x1, Pallas kernels, local(): pl.pallas_call(functools.partial(kernel, chips, owners, heads), out_shape...  68.3 us

profile of v8, /device:TPU:65, one launch (start us, length us, event | category | flops | bytes accessed | tf_op | source)
XLA Modules:
  0.0 68.9 jit_solution(7551914720683474897)
XLA Ops:
  0.0 68.3 %shard_map.82 = bf16[8,448]{1,0:T(8,128)(2,1)S(1)} custom-call(bf16[2,896]{1,0:T(2,128)(2,1)} %q_hbm.1, bf16[4,256,896]{2,1,0:T(8,128)(2,1)} %k_hbm.1, bf16[4,256,896]{2,1,0:T(8,128)(2,1)} %v_hbm.1, f32[7]{0:T(128)} %slopes_hbm.1, s32[4]{0:T(128)} %block_seq_hbm.1, s32[4]{0:T(128)} %block_pos_hbm.1, s32[64]{0:T(128)} %lengths_hbm.1, bf16[448,896]{1,0:T(8,128)(2,1)} %bitcast.1), custom_call_target="tpu_custom_call" | custom-call | tf_op jit(solution)/shard_map/pallas_call | solution.py:393
  68.3 0.6 copy.10
